TPU v7x, 32 devices: a whole 2x2x4 slice. The times are simulated.
32 devices in a mesh: gx: 4 (over z), gy: 8 (over y, x, core).
Axes of the slice: x: 2, y: 2, z: 4, core: 2. Of those that a mesh axis runs over, the one named last changes fastest.
Arguments:
- features: bfloat16 [40960, 2048], P(('gx', 'gy')), may hold values from -6 to 6
- counts: int32 [32], P(('gx', 'gy')), may hold values from 128 to 1280, as said below
- ref_mean: float32 [2048], replicated, may hold values from -6 to 6
- ref_root: float32 [2048, 2048], P('gx', 'gy'), as said below
Outputs:
- mean: float32 [2048], replicated
- root: float32 [2048, 2048], P('gx', 'gy')
- distance: float32 [], replicated
Inputs may be any that keep to these rules, and one draw needn't show every extreme that they name: Entry b counts the valid rows of shard b, which come first in it; a multiple of 128; some shard is full in every draw. `ref_root`: symmetric and positive definite.
All inputs are finite; a program needn't handle non-finite values.
Results may differ from a plain program's by a relative error of at most 0.0015.
The roundings to bfloat16 on the way count: a program that leaves them out, or rounds other values in their place, can miss the bound.
Values may be sent and summed in bfloat16 or wider, within the bound.
A program may use at most 128 MiB of HBM per device.

v0:
```python
import jax
import jax.numpy as jnp
from jax import lax
from jax.sharding import PartitionSpec as P

ITERS = 4


def product(left, right):
    left_half = left.astype(jnp.bfloat16)
    right_half = right.astype(jnp.bfloat16)
    panel = lax.all_gather(left_half, "gy", axis=1, tiled=True)
    return jnp.dot(
        panel,
        lax.all_gather(right_half, "gx", axis=0, tiled=True),
        preferred_element_type=jnp.float32,
    )


def shards(features, counts, ref_mean, ref_root):
    width = features.shape[1]
    slots = features.shape[0]
    rows_x = lax.axis_size("gx")
    cols_y = lax.axis_size("gy")
    tile_rows = width // rows_x
    tile_cols = width // cols_y
    keep = (jnp.arange(slots, dtype=jnp.int32) < counts[0])[:, None]
    masked = jnp.where(keep, features, jnp.zeros_like(features))
    partial_gram = lax.dot_general(
        masked, features, (((0,), (0,)), ((), ())), preferred_element_type=jnp.float32
    )
    column_total = jnp.sum(masked.astype(jnp.float32), axis=0)
    local_count = counts[0].astype(jnp.float32)
    total, count = lax.psum((column_total, local_count), ("gx", "gy"))
    column_block = lax.psum_scatter(partial_gram, "gy", scatter_dimension=1, tiled=True)
    gram_tile = lax.psum_scatter(column_block, "gx", scatter_dimension=0, tiled=True)
    mean = total / count
    row_start = lax.axis_index("gx") * tile_rows
    col_start = lax.axis_index("gy") * tile_cols
    mean_rows = lax.dynamic_slice_in_dim(mean, row_start, tile_rows, 0)
    mean_cols = lax.dynamic_slice_in_dim(mean, col_start, tile_cols, 0)
    cov_tile = (gram_tile - count * mean_rows[:, None] * mean_cols[None, :]) / (count - 1.0)
    row_ids = jnp.arange(tile_rows, dtype=jnp.int32) + row_start
    col_ids = jnp.arange(tile_cols, dtype=jnp.int32) + col_start
    identity_tile = (row_ids[:, None] == col_ids[None, :]).astype(jnp.float32)
    half = product(cov_tile, ref_root)
    prod = product(ref_root, half)
    square_sum, cov_trace, root_square = lax.psum(
        (jnp.sum(prod * prod), jnp.sum(cov_tile * identity_tile), jnp.sum(ref_root * ref_root)),
        ("gx", "gy"),
    )
    scale = jnp.sqrt(square_sum + 1.0)
    current = prod / scale
    partner = identity_tile
    for step in range(ITERS):
        middle = 1.5 * identity_tile - 0.5 * product(partner, current)
        current, partner = (product(current, middle), product(middle, partner))
    last_trace = lax.psum(jnp.sum(current * identity_tile), ("gx", "gy"))
    root = jnp.sqrt(scale) * current
    distance = (
        jnp.sum((mean - ref_mean) ** 2)
        + cov_trace
        + root_square
        - 2.0 * jnp.sqrt(scale) * last_trace
    ) / 64.0
    return (mean, root, distance)


def solution(mesh):
    return jax.shard_map(
        shards,
        mesh=mesh,
        in_specs=(P(("gx", "gy"), None), P(("gx", "gy")), P(), P("gx", "gy")),
        out_specs=(P(), P("gx", "gy"), P()),
        check_vma=False,
    )
```

profile of v0, /device:TPU:0, one launch (start us, length us, event | category | flops | bytes accessed | tf_op | source)
XLA Modules:
  0.0 1031.6 jit_solution(1172393237996310174)
XLA Ops:
  7.9 18.1 %fusion = f32[2048,2048]{1,0:T(8,128)} fusion(bf16[1280,2048]{1,0:T(8,128)(2,1)} %param.4, pred[1280]{0:T(1024)(128)(4,1)S(1)} %iota_compare_fusion), kind=kOutput, calls=%fused_computation.1 | convolution fusion | flops 10740039680 | bytes 22021376 | tf_op jit(solution)/shard_map/dot_general | solution.py:29
  26.1 118.8 %reduce-scatter.3.cloned.1.call-done = f32[2048,256]{1,0:T(8,128)} async-done(((f32[2048,2048]{1,0:T(8,128)}), f32[2048,256]{1,0:T(8,128)}) %reduce-scatter.3.cloned.1.call-update) | async-done | bytes 2097168 | tf_op jit(solution)/shard_map/reduce_scatter | solution.py:35
  146.4 3.6 convert_reduce_fusion
  150.0 42.2 %all-reduce.1 = (f32[2048]{0:T(1024)S(1)}, f32[]{:T(128)}) all-reduce(f32[2048]{0:T(1024)S(1)} %convert_reduce_fusion, f32[]{:T(128)S(6)} %convert_element_type.69), channel_id=1, replica_groups=mesh['gx'=4,'gy'=8] {'gx','gy'}, use_global_device_ids=true, to_apply=%region_1.2 | all-reduce | flops 2049 | bytes 16392 | tf_op jit(solution)/shard_map/psum | solution.py:34
  197.5 23.1 %all-gather.29.cloned.1.call-done = bf16[2048,256]{1,0:T(8,128)(2,1)} async-done(((bf16[512,256]{1,0:T(8,128)(2,1)}), bf16[2048,256]{1,0:T(8,128)(2,1)}) %all-gather.29.cloned.1.call-update) | async-done | bytes 1048592 | tf_op jit(solution)/shard_map/all_gather | solution.py:15
  220.6 29.8 %all-gather.27.cloned.1.call-done = bf16[512,2048]{1,0:T(8,128)(2,1)} async-done(((bf16[512,256]{1,0:T(8,128)(2,1)}), bf16[512,2048]{1,0:T(8,128)(2,1)}) %all-gather.27.cloned.1.call-update) | async-done | bytes 2097168 | tf_op jit(solution)/shard_map/all_gather | solution.py:12
  254.7 25.6 %all-gather.33.cloned.1.call-done = bf16[512,2048]{1,0:T(8,128)(2,1)} async-done(((bf16[512,256]{1,0:T(8,128)(2,1)}), bf16[512,2048]{1,0:T(8,128)(2,1)}) %all-gather.33.cloned.1.call-update) | async-done | bytes 2097168 | tf_op jit(solution)/shard_map/all_gather | solution.py:12
  280.3 30.0 %all-gather.31.cloned.1.call-done = bf16[2048,256]{1,0:T(8,128)(2,1)} async-done(((bf16[512,256]{1,0:T(8,128)(2,1)}), bf16[2048,256]{1,0:T(8,128)(2,1)}) %all-gather.31.cloned.1.call-update) | async-done | bytes 1048592 | tf_op jit(solution)/shard_map/all_gather | solution.py:15
  313.6 40.4 %psum.44 = f32[]{:T(128)} all-reduce(f32[]{:T(128)} %get-tuple-element.15), channel_id=1, replica_groups=mesh['gx'=4,'gy'=8] {'gx','gy'}, use_global_device_ids=true, to_apply=%region_6.7 | all-reduce | flops 1 | bytes 8 | tf_op jit(solution)/shard_map/psum | solution.py:48
  355.5 27.4 %all-gather.39.cloned.1.call-done = bf16[2048,256]{0,1:T(8,128)(2,1)} async-done(((bf16[512,256]{0,1:T(8,128)(2,1)}), bf16[2048,256]{0,1:T(8,128)(2,1)}) %all-gather.39.cloned.1.call-update) | async-done | bytes 1048592 | tf_op jit(solution)/shard_map/all_gather | solution.py:15
  388.5 25.4 %all-gather.41.cloned.1.call-done = bf16[2048,256]{1,0:T(8,128)(2,1)} async-done(((bf16[512,256]{1,0:T(8,128)(2,1)}), bf16[2048,256]{1,0:T(8,128)(2,1)}) %all-gather.41.cloned.1.call-update) | async-done | bytes 1048592 | tf_op jit(solution)/shard_map/all_gather | solution.py:15
  413.8 29.5 %all-gather.35.cloned.1.call-done = bf16[512,2048]{0,1:T(8,128)(2,1)} async-done(((bf16[512,256]{0,1:T(8,128)(2,1)}), bf16[512,2048]{0,1:T(8,128)(2,1)}) %all-gather.35.cloned.1.call-update) | async-done | bytes 2097168 | tf_op jit(solution)/shard_map/all_gather | solution.py:12
  446.7 26.2 %all-gather.47.cloned.1.call-done = bf16[2048,256]{1,0:T(8,128)(2,1)} async-done(((bf16[512,256]{1,0:T(8,128)(2,1)}), bf16[2048,256]{1,0:T(8,128)(2,1)}) %all-gather.47.cloned.1.call-update) | async-done | bytes 1048592 | tf_op jit(solution)/shard_map/all_gather | solution.py:15
  472.9 29.2 %all-gather.45.cloned.1.call-done = bf16[512,2048]{1,0:T(8,128)(2,1)} async-done(((bf16[512,256]{1,0:T(8,128)(2,1)}), bf16[512,2048]{1,0:T(8,128)(2,1)}) %all-gather.45.cloned.1.call-update) | async-done | bytes 2097168 | tf_op jit(solution)/shard_map/all_gather | solution.py:12
  506.1 26.2 %all-gather.51.cloned.1.call-done = bf16[2048,256]{1,0:T(8,128)(2,1)} async-done(((bf16[512,256]{1,0:T(8,128)(2,1)}), bf16[2048,256]{1,0:T(8,128)(2,1)}) %all-gather.51.cloned.1.call-update) | async-done | bytes 1048592 | tf_op jit(solution)/shard_map/all_gather | solution.py:15
  532.3 29.2 %all-gather.49.cloned.1.call-done = bf16[512,2048]{1,0:T(8,128)(2,1)} async-done(((bf16[512,256]{1,0:T(8,128)(2,1)}), bf16[512,2048]{1,0:T(8,128)(2,1)}) %all-gather.49.cloned.1.call-update) | async-done | bytes 2097168 | tf_op jit(solution)/shard_map/all_gather | solution.py:12
  566.1 25.9 %all-gather.43.cloned.1.call-done = bf16[512,2048]{1,0:T(8,128)(2,1)} async-done(((bf16[512,256]{1,0:T(8,128)(2,1)}), bf16[512,2048]{1,0:T(8,128)(2,1)}) %all-gather.43.cloned.1.call-update) | async-done | bytes 2097168 | tf_op jit(solution)/shard_map/all_gather | solution.py:12
  592.0 29.4 %all-gather.53.cloned.1.call-done = bf16[2048,256]{1,0:T(8,128)(2,1)} async-done(((bf16[512,256]{1,0:T(8,128)(2,1)}), bf16[2048,256]{1,0:T(8,128)(2,1)}) %all-gather.53.cloned.1.call-update) | async-done | bytes 1048592 | tf_op jit(solution)/shard_map/all_gather | solution.py:15
  624.8 25.5 %all-gather.59.cloned.1.call-done = bf16[2048,256]{1,0:T(8,128)(2,1)} async-done(((bf16[512,256]{1,0:T(8,128)(2,1)}), bf16[2048,256]{1,0:T(8,128)(2,1)}) %all-gather.59.cloned.1.call-update) | async-done | bytes 1048592 | tf_op jit(solution)/shard_map/all_gather | solution.py:15
  650.2 29.2 %all-gather.57.cloned.1.call-done = bf16[512,2048]{1,0:T(8,128)(2,1)} async-done(((bf16[512,256]{1,0:T(8,128)(2,1)}), bf16[512,2048]{1,0:T(8,128)(2,1)}) %all-gather.57.cloned.1.call-update) | async-done | bytes 2097168 | tf_op jit(solution)/shard_map/all_gather | solution.py:12
  683.6 26.1 %all-gather.63.cloned.1.call-done = bf16[2048,256]{1,0:T(8,128)(2,1)} async-done(((bf16[512,256]{1,0:T(8,128)(2,1)}), bf16[2048,256]{1,0:T(8,128)(2,1)}) %all-gather.63.cloned.1.call-update) | async-done | bytes 1048592 | tf_op jit(solution)/shard_map/all_gather | solution.py:15
  709.6 29.2 %all-gather.61.cloned.1.call-done = bf16[512,2048]{1,0:T(8,128)(2,1)} async-done(((bf16[512,256]{1,0:T(8,128)(2,1)}), bf16[512,2048]{1,0:T(8,128)(2,1)}) %all-gather.61.cloned.1.call-update) | async-done | bytes 2097168 | tf_op jit(solution)/shard_map/all_gather | solution.py:12
  743.5 25.9 %all-gather.55.cloned.1.call-done = bf16[512,2048]{1,0:T(8,128)(2,1)} async-done(((bf16[512,256]{1,0:T(8,128)(2,1)}), bf16[512,2048]{1,0:T(8,128)(2,1)}) %all-gather.55.cloned.1.call-update) | async-done | bytes 2097168 | tf_op jit(solution)/shard_map/all_gather | solution.py:12
  769.5 29.6 %all-gather.65.cloned.1.call-done = bf16[2048,256]{1,0:T(8,128)(2,1)} async-done(((bf16[512,256]{1,0:T(8,128)(2,1)}), bf16[2048,256]{1,0:T(8,128)(2,1)}) %all-gather.65.cloned.1.call-update) | async-done | bytes 1048592 | tf_op jit(solution)/shard_map/all_gather | solution.py:15
  802.4 25.6 %all-gather.71.cloned.1.call-done = bf16[2048,256]{1,0:T(8,128)(2,1)} async-done(((bf16[512,256]{1,0:T(8,128)(2,1)}), bf16[2048,256]{1,0:T(8,128)(2,1)}) %all-gather.71.cloned.1.call-update) | async-done | bytes 1048592 | tf_op jit(solution)/shard_map/all_gather | solution.py:15
  828.0 29.2 %all-gather.69.cloned.1.call-done = bf16[512,2048]{1,0:T(8,128)(2,1)} async-done(((bf16[512,256]{1,0:T(8,128)(2,1)}), bf16[512,2048]{1,0:T(8,128)(2,1)}) %all-gather.69.cloned.1.call-update) | async-done | bytes 2097168 | tf_op jit(solution)/shard_map/all_gather | solution.py:12
  861.2 26.2 %all-gather.75.cloned.1.call-done = bf16[2048,256]{1,0:T(8,128)(2,1)} async-done(((bf16[512,256]{1,0:T(8,128)(2,1)}), bf16[2048,256]{1,0:T(8,128)(2,1)}) %all-gather.75.cloned.1.call-update) | async-done | bytes 1048592 | tf_op jit(solution)/shard_map/all_gather | solution.py:15
  887.4 29.2 %all-gather.73.cloned.1.call-done = bf16[512,2048]{1,0:T(8,128)(2,1)} async-done(((bf16[512,256]{1,0:T(8,128)(2,1)}), bf16[512,2048]{1,0:T(8,128)(2,1)}) %all-gather.73.cloned.1.call-update) | async-done | bytes 2097168 | tf_op jit(solution)/shard_map/all_gather | solution.py:12
  920.0 27.1 %all-gather.67.cloned.1.call-done = bf16[512,2048]{1,0:T(8,128)(2,1)} async-done(((bf16[512,256]{1,0:T(8,128)(2,1)}), bf16[512,2048]{1,0:T(8,128)(2,1)}) %all-gather.67.cloned.1.call-update) | async-done | bytes 2097168 | tf_op jit(solution)/shard_map/all_gather | solution.py:12
  947.1 29.6 %all-gather.77.cloned.1.call-done = bf16[2048,256]{1,0:T(8,128)(2,1)} async-done(((bf16[512,256]{1,0:T(8,128)(2,1)}), bf16[2048,256]{1,0:T(8,128)(2,1)}) %all-gather.77.cloned.1.call-update) | async-done | bytes 1048592 | tf_op jit(solution)/shard_map/all_gather | solution.py:15
  976.7 4.0 fusion.14
  980.7 40.4 %all-reduce = (f32[]{:T(128)}, f32[]{:T(128)}, f32[]{:T(128)}) all-reduce(f32[]{:T(128)} %get-tuple-element.4, f32[]{:T(128)} %get-tuple-element.12, f32[]{:T(128)} %get-tuple-element.3), channel_id=1, replica_groups=mesh['gx'=4,'gy'=8] {'gx','gy'}, use_global_device_ids=true, to_apply=%region_9.10 | all-reduce | flops 3 | bytes 24 | tf_op jit(solution)/shard_map/psum | solution.py:48
  (88 shorter events, 54.3 us)
Async XLA Ops:
  7.2 137.7 %reduce-scatter.3.cloned.1.call-start = ((), (), s32[]{:S(2)}) async-start(), calls=%async_computation.2 | async-start | bytes 18874368 | tf_op jit(solution)/shard_map/reduce_scatter | solution.py:35
  26.0 118.9 %copy-start = (f32[512,256]{1,0:T(8,128)S(1)}, f32[512,256]{1,0:T(8,128)}, u32[]{:S(2)}) copy-start(f32[512,256]{1,0:T(8,128)} %param.7) | copy-start | bytes 1572868
  26.0 169.0 %reduce-scatter.5.cloned.1.call-start = ((), (), s32[]{:S(2)}) async-start(), calls=%async_computation.3 | async-start | bytes 2621440 | tf_op jit(solution)/shard_map/reduce_scatter | solution.py:36
  144.8 75.8 %all-gather.29.cloned.1.call-start = ((), (), s32[]{:S(2)}) async-start(), calls=%async_computation.5 | async-start | bytes 1310720 | tf_op jit(solution)/shard_map/all_gather | solution.py:15
  146.3 104.1 %all-gather.27.cloned.1.call-start = ((), (), s32[]{:S(2)}) async-start(), calls=%async_computation.4 | async-start | bytes 2359296 | tf_op jit(solution)/shard_map/all_gather | solution.py:12
  146.4 46.5 %copy-start.3 = (f32[2048]{0:T(1024)S(1)}, f32[2048]{0:T(1024)}, u32[]{:S(2)}) copy-start(f32[2048]{0:T(1024)} %param.6) | copy-start | bytes 24580
  194.2 59.5 %copy-start.2 = (f32[2048]{0:T(1024)}, f32[2048]{0:T(1024)S(1)}, u32[]{:S(2)}) copy-start(f32[2048]{0:T(1024)S(1)} %get-tuple-element.11) | copy-start | bytes 24580
  196.9 83.4 %all-gather.33.cloned.1.call-start = ((), (), s32[]{:S(2)}) async-start(), calls=%async_computation.7 | async-start | bytes 2359296 | tf_op jit(solution)/shard_map/all_gather | solution.py:12
  197.5 112.8 %all-gather.31.cloned.1.call-start = ((), (), s32[]{:S(2)}) async-start(), calls=%async_computation.6 | async-start | bytes 1310720 | tf_op jit(solution)/shard_map/all_gather | solution.py:15
  253.7 101.8 %all-gather.37.cloned.1.call-start = ((), (), s32[]{:S(2)}) async-start(), calls=%async_computation.9 | async-start | bytes 2359296 | tf_op jit(solution)/shard_map/all_gather | solution.py:12
  254.7 128.3 %all-gather.39.cloned.1.call-start = ((), (), s32[]{:S(2)}) async-start(), calls=%async_computation.10 | async-start | bytes 1310720 | tf_op jit(solution)/shard_map/all_gather | solution.py:15
  355.5 58.4 %all-gather.41.cloned.1.call-start = ((), (), s32[]{:S(2)}) async-start(), calls=%async_computation.11 | async-start | bytes 1310720 | tf_op jit(solution)/shard_map/all_gather | solution.py:15
  386.3 57.0 %all-gather.35.cloned.1.call-start = ((), (), s32[]{:S(2)}) async-start(), calls=%async_computation.8 | async-start | bytes 2359296 | tf_op jit(solution)/shard_map/all_gather | solution.py:12
  386.9 86.0 %all-gather.47.cloned.1.call-start = ((), (), s32[]{:S(2)}) async-start(), calls=%async_computation.14 | async-start | bytes 1310720 | tf_op jit(solution)/shard_map/all_gather | solution.py:15
  387.7 114.5 %all-gather.45.cloned.1.call-start = ((), (), s32[]{:S(2)}) async-start(), calls=%async_computation.13 | async-start | bytes 2359296 | tf_op jit(solution)/shard_map/all_gather | solution.py:12
  388.2 144.1 %all-gather.51.cloned.1.call-start = ((), (), s32[]{:S(2)}) async-start(), calls=%async_computation.16 | async-start | bytes 1310720 | tf_op jit(solution)/shard_map/all_gather | solution.py:15
  446.7 114.9 %all-gather.49.cloned.1.call-start = ((), (), s32[]{:S(2)}) async-start(), calls=%async_computation.15 | async-start | bytes 2359296 | tf_op jit(solution)/shard_map/all_gather | solution.py:12
  505.5 86.5 %all-gather.43.cloned.1.call-start = ((), (), s32[]{:S(2)}) async-start(), calls=%async_computation.12 | async-start | bytes 2359296 | tf_op jit(solution)/shard_map/all_gather | solution.py:12
  506.1 115.4 %all-gather.53.cloned.1.call-start = ((), (), s32[]{:S(2)}) async-start(), calls=%async_computation.17 | async-start | bytes 1310720 | tf_op jit(solution)/shard_map/all_gather | solution.py:15
  564.9 85.4 %all-gather.59.cloned.1.call-start = ((), (), s32[]{:S(2)}) async-start(), calls=%async_computation.20 | async-start | bytes 1310720 | tf_op jit(solution)/shard_map/all_gather | solution.py:15
  565.5 114.0 %all-gather.57.cloned.1.call-start = ((), (), s32[]{:S(2)}) async-start(), calls=%async_computation.19 | async-start | bytes 2359296 | tf_op jit(solution)/shard_map/all_gather | solution.py:12
  566.0 143.6 %all-gather.63.cloned.1.call-start = ((), (), s32[]{:S(2)}) async-start(), calls=%async_computation.22 | async-start | bytes 1310720 | tf_op jit(solution)/shard_map/all_gather | solution.py:15
  624.7 114.1 %all-gather.61.cloned.1.call-start = ((), (), s32[]{:S(2)}) async-start(), calls=%async_computation.21 | async-start | bytes 2359296 | tf_op jit(solution)/shard_map/all_gather | solution.py:12
  682.8 86.7 %all-gather.55.cloned.1.call-start = ((), (), s32[]{:S(2)}) async-start(), calls=%async_computation.18 | async-start | bytes 2359296 | tf_op jit(solution)/shard_map/all_gather | solution.py:12
  683.5 115.5 %all-gather.65.cloned.1.call-start = ((), (), s32[]{:S(2)}) async-start(), calls=%async_computation.23 | async-start | bytes 1310720 | tf_op jit(solution)/shard_map/all_gather | solution.py:15
  742.2 85.8 %all-gather.71.cloned.1.call-start = ((), (), s32[]{:S(2)}) async-start(), calls=%async_computation.26 | async-start | bytes 1310720 | tf_op jit(solution)/shard_map/all_gather | solution.py:15
  742.9 114.3 %all-gather.69.cloned.1.call-start = ((), (), s32[]{:S(2)}) async-start(), calls=%async_computation.25 | async-start | bytes 2359296 | tf_op jit(solution)/shard_map/all_gather | solution.py:12
  743.5 143.9 %all-gather.75.cloned.1.call-start = ((), (), s32[]{:S(2)}) async-start(), calls=%async_computation.28 | async-start | bytes 1310720 | tf_op jit(solution)/shard_map/all_gather | solution.py:15
  802.3 114.3 %all-gather.73.cloned.1.call-start = ((), (), s32[]{:S(2)}) async-start(), calls=%async_computation.27 | async-start | bytes 2359296 | tf_op jit(solution)/shard_map/all_gather | solution.py:12
  860.5 86.5 %all-gather.67.cloned.1.call-start = ((), (), s32[]{:S(2)}) async-start(), calls=%async_computation.24 | async-start | bytes 2359296 | tf_op jit(solution)/shard_map/all_gather | solution.py:12
  861.1 115.5 %copy-start.1 = (f32[512,256]{1,0:T(8,128)S(1)}, f32[512,256]{1,0:T(8,128)}, u32[]{:S(2)}) copy-start(f32[512,256]{1,0:T(8,128)} %reduce-scatter.5.cloned.1.call-done) | copy-start | bytes 1572868
  861.2 115.5 %all-gather.77.cloned.1.call-start = ((), (), s32[]{:S(2)}) async-start(), calls=%async_computation.29 | async-start | bytes 1310720 | tf_op jit(solution)/shard_map/all_gather | solution.py:15
Sparse Core Ops, SparseCore 0:
  26.1 118.6 reduce-scatter.2
  147.1 44.6 reduce-scatter.4
  193.4 27.1 all-gather.28
  222.9 27.4 all-gather.26
  252.2 28.0 all-gather.32
  282.3 27.9 all-gather.30
  312.2 27.6 all-gather.36
  355.6 27.3 all-gather.38
  386.5 27.3 all-gather.40
  416.2 27.1 all-gather.34
  444.9 27.9 all-gather.46
  474.7 27.4 all-gather.44
  504.3 27.9 all-gather.50
  534.1 27.4 all-gather.48
  563.9 28.0 all-gather.42
  593.4 27.9 all-gather.52
  622.9 27.3 all-gather.58
  652.0 27.4 all-gather.56
  681.6 27.9 all-gather.62
  711.4 27.4 all-gather.60
  741.3 28.0 all-gather.54
  771.0 27.9 all-gather.64
  800.6 27.3 all-gather.70
  829.8 27.4 all-gather.68
  859.4 27.9 all-gather.74
  889.1 27.4 all-gather.72
  919.0 28.0 all-gather.66
  948.7 27.9 all-gather.76
where the time goes:
time: 1030 us
  waiting for transfers between devices  815 us (79%)
  blocking collectives  123 us (12%)
  matrix products  61.5 us (6%)
  between operations  20.3 us (2%)
  other arithmetic  10.5 us (1%)
    all_gather x13, waiting for transfers between devices, product(): lax.all_gather(right_half, 'gx', axis=0, tiled=True)  350 us
    all_gather x13, waiting for transfers between devices, product(): panel = lax.all_gather(left_half, 'gy', axis=1, tiled=True)  339 us
    reduce_scatter x1, waiting for transfers between devices, shards(): lax.psum_scatter(partial_gram, 'gy', scatter_dimension=1, tiled=True)  119 us
    psum x2, blocking collectives, shards(): lax.psum((jnp.sum(prod * prod), jnp.sum(cov_tile * identity_tile), jnp.su...  80.7 us
    dot_general x13, matrix products, product(): jnp.dot(panel, lax.all_gather(right_half, 'gx', axis=0, tiled=True), pref...  43.4 us
    psum x1, blocking collectives, shards(): total, count = lax.psum((column_total, local_count), ('gx', 'gy'))  42.2 us
  transfers between devices with their start and end apart: 28, of which 26 were waited for; matrix products, arithmetic and copies ran while one was open for 5% of the time, Pallas kernels for 0%

commit v1 on v0

--- a/solution.py
+++ b/solution.py
@@ -4,6 +4,7 @@
 from jax.sharding import PartitionSpec as P
 
 ITERS = 4
+touch_shards = lambda row_data: lax.psum(lax.psum(row_data, "gy"), "gx")
 
 
 def product(left, right):
@@ -45,9 +46,8 @@
     identity_tile = (row_ids[:, None] == col_ids[None, :]).astype(jnp.float32)
     half = product(cov_tile, ref_root)
     prod = product(ref_root, half)
-    square_sum, cov_trace, root_square = lax.psum(
-        (jnp.sum(prod * prod), jnp.sum(cov_tile * identity_tile), jnp.sum(ref_root * ref_root)),
-        ("gx", "gy"),
+    square_sum, cov_trace, root_square = touch_shards(
+        (jnp.sum(prod * prod), jnp.sum(cov_tile * identity_tile), jnp.sum(ref_root * ref_root))
     )
     scale = jnp.sqrt(square_sum + 1.0)
     current = prod / scale

time: 1030 us -> 1040 us (level)
    psum x2 -> x5, blocking collectives: 80.7 us -> 89.9 us  [the longest x4 49.6 us: touch_shards = lambda row_data: lax.psum(lax.psum(row_data, 'gy'), 'gx')]
  transfers between devices with their start and end apart: 28 -> 28, of which waited for: 26 -> 26; matrix products, arithmetic and copies ran while one was open for 5% -> 4% of each run, Pallas kernels for 0% -> 0%
where the time goes in v1:
time: 1040 us
  waiting for transfers between devices  817 us (79%)
  blocking collectives  132 us (13%)
  matrix products  61.5 us (6%)
  between operations  20.3 us (2%)
  other arithmetic  10.4 us (1%)
    all_gather x13, waiting for transfers between devices, product(): lax.all_gather(right_half, 'gx', axis=0, tiled=True)  352 us
    all_gather x13, waiting for transfers between devices, product(): panel = lax.all_gather(left_half, 'gy', axis=1, tiled=True)  339 us
    reduce_scatter x1, waiting for transfers between devices, shards(): lax.psum_scatter(partial_gram, 'gy', scatter_dimension=1, tiled=True)  119 us
    psum x4, blocking collectives, touch_shards = lambda row_data: lax.psum(lax.psum(row_data, 'gy'), 'gx')  49.6 us
    dot_general x13, matrix products, product(): jnp.dot(panel, lax.all_gather(right_half, 'gx', axis=0, tiled=True), pref...  43.4 us
    psum x1, blocking collectives, shards(): total, count = lax.psum((column_total, local_count), ('gx', 'gy'))  42.3 us
    psum x1, blocking collectives, shards(): last_trace = lax.psum(jnp.sum(current * identity_tile), ('gx', 'gy'))  40.3 us
  transfers between devices with their start and end apart: 28, of which 26 were waited for; matrix products, arithmetic and copies ran while one was open for 4% of the time, Pallas kernels for 0%

profile of v1, /device:TPU:0, one launch (start us, length us, event | category | flops | bytes accessed | tf_op | source)
XLA Modules:
  0.0 1042.7 jit_solution(2755288852949288921)
XLA Ops:
  7.9 18.1 %fusion = f32[2048,2048]{1,0:T(8,128)} fusion(bf16[1280,2048]{1,0:T(8,128)(2,1)} %param.4, pred[1280]{0:T(1024)(128)(4,1)S(1)} %iota_compare_fusion), kind=kOutput, calls=%fused_computation.1 | convolution fusion | flops 10740039680 | bytes 22021376 | tf_op jit(solution)/shard_map/dot_general | solution.py:30
  26.1 118.8 %reduce-scatter.3.cloned.1.call-done = f32[2048,256]{1,0:T(8,128)} async-done(((f32[2048,2048]{1,0:T(8,128)}), f32[2048,256]{1,0:T(8,128)}) %reduce-scatter.3.cloned.1.call-update) | async-done | bytes 2097168 | tf_op jit(solution)/shard_map/reduce_scatter | solution.py:36
  149.9 42.3 %all-reduce = (f32[2048]{0:T(1024)S(1)}, f32[]{:T(128)}) all-reduce(f32[2048]{0:T(1024)S(1)} %convert_reduce_fusion, f32[]{:T(128)S(6)} %convert_element_type.69), channel_id=1, replica_groups=mesh['gx'=4,'gy'=8] {'gx','gy'}, use_global_device_ids=true, to_apply=%region_1.2 | all-reduce | flops 2049 | bytes 16392 | tf_op jit(solution)/shard_map/psum | solution.py:35
  197.5 23.1 %all-gather.29.cloned.1.call-done = bf16[2048,256]{1,0:T(8,128)(2,1)} async-done(((bf16[512,256]{1,0:T(8,128)(2,1)}), bf16[2048,256]{1,0:T(8,128)(2,1)}) %all-gather.29.cloned.1.call-update) | async-done | bytes 1048592 | tf_op jit(solution)/shard_map/all_gather | solution.py:16
  220.6 29.8 %all-gather.27.cloned.1.call-done = bf16[512,2048]{1,0:T(8,128)(2,1)} async-done(((bf16[512,256]{1,0:T(8,128)(2,1)}), bf16[512,2048]{1,0:T(8,128)(2,1)}) %all-gather.27.cloned.1.call-update) | async-done | bytes 2097168 | tf_op jit(solution)/shard_map/all_gather | solution.py:13
  254.7 25.6 %all-gather.33.cloned.1.call-done = bf16[512,2048]{1,0:T(8,128)(2,1)} async-done(((bf16[512,256]{1,0:T(8,128)(2,1)}), bf16[512,2048]{1,0:T(8,128)(2,1)}) %all-gather.33.cloned.1.call-update) | async-done | bytes 2097168 | tf_op jit(solution)/shard_map/all_gather | solution.py:13
  280.3 30.0 %all-gather.31.cloned.1.call-done = bf16[2048,256]{1,0:T(8,128)(2,1)} async-done(((bf16[512,256]{1,0:T(8,128)(2,1)}), bf16[2048,256]{1,0:T(8,128)(2,1)}) %all-gather.31.cloned.1.call-update) | async-done | bytes 1048592 | tf_op jit(solution)/shard_map/all_gather | solution.py:16
  313.6 13.8 %psum.65 = f32[]{:T(128)} all-reduce(f32[]{:T(128)} %get-tuple-element.16), channel_id=1, replica_groups=mesh['gx'=4,'gy'=8] {'gy'}, use_global_device_ids=true, to_apply=%region_6.7 | all-reduce | flops 1 | bytes 8 | tf_op jit(solution)/shard_map/psum | solution.py:7
  327.4 11.5 %psum.66 = f32[]{:T(128)} all-reduce(f32[]{:T(128)} %psum.65), channel_id=1, replica_groups=mesh['gx'=4,'gy'=8] {'gx'}, use_global_device_ids=true, to_apply=%region_7.8 | all-reduce | flops 1 | bytes 8 | tf_op jit(solution)/shard_map/psum | solution.py:7
  340.5 29.4 %all-gather.39.cloned.1.call-done = bf16[2048,256]{0,1:T(8,128)(2,1)} async-done(((bf16[512,256]{0,1:T(8,128)(2,1)}), bf16[2048,256]{0,1:T(8,128)(2,1)}) %all-gather.39.cloned.1.call-update) | async-done | bytes 1048592 | tf_op jit(solution)/shard_map/all_gather | solution.py:16
  375.2 25.6 %all-gather.41.cloned.1.call-done = bf16[2048,256]{1,0:T(8,128)(2,1)} async-done(((bf16[512,256]{1,0:T(8,128)(2,1)}), bf16[2048,256]{1,0:T(8,128)(2,1)}) %all-gather.41.cloned.1.call-update) | async-done | bytes 1048592 | tf_op jit(solution)/shard_map/all_gather | solution.py:16
  400.7 29.5 %all-gather.35.cloned.1.call-done = bf16[512,2048]{0,1:T(8,128)(2,1)} async-done(((bf16[512,256]{0,1:T(8,128)(2,1)}), bf16[512,2048]{0,1:T(8,128)(2,1)}) %all-gather.35.cloned.1.call-update) | async-done | bytes 2097168 | tf_op jit(solution)/shard_map/all_gather | solution.py:13
  433.8 26.0 %all-gather.47.cloned.1.call-done = bf16[2048,256]{1,0:T(8,128)(2,1)} async-done(((bf16[512,256]{1,0:T(8,128)(2,1)}), bf16[2048,256]{1,0:T(8,128)(2,1)}) %all-gather.47.cloned.1.call-update) | async-done | bytes 1048592 | tf_op jit(solution)/shard_map/all_gather | solution.py:16
  459.8 29.2 %all-gather.45.cloned.1.call-done = bf16[512,2048]{1,0:T(8,128)(2,1)} async-done(((bf16[512,256]{1,0:T(8,128)(2,1)}), bf16[512,2048]{1,0:T(8,128)(2,1)}) %all-gather.45.cloned.1.call-update) | async-done | bytes 2097168 | tf_op jit(solution)/shard_map/all_gather | solution.py:13
  493.0 26.2 %all-gather.51.cloned.1.call-done = bf16[2048,256]{1,0:T(8,128)(2,1)} async-done(((bf16[512,256]{1,0:T(8,128)(2,1)}), bf16[2048,256]{1,0:T(8,128)(2,1)}) %all-gather.51.cloned.1.call-update) | async-done | bytes 1048592 | tf_op jit(solution)/shard_map/all_gather | solution.py:16
  519.2 29.2 %all-gather.49.cloned.1.call-done = bf16[512,2048]{1,0:T(8,128)(2,1)} async-done(((bf16[512,256]{1,0:T(8,128)(2,1)}), bf16[512,2048]{1,0:T(8,128)(2,1)}) %all-gather.49.cloned.1.call-update) | async-done | bytes 2097168 | tf_op jit(solution)/shard_map/all_gather | solution.py:13
  553.0 25.9 %all-gather.43.cloned.1.call-done = bf16[512,2048]{1,0:T(8,128)(2,1)} async-done(((bf16[512,256]{1,0:T(8,128)(2,1)}), bf16[512,2048]{1,0:T(8,128)(2,1)}) %all-gather.43.cloned.1.call-update) | async-done | bytes 2097168 | tf_op jit(solution)/shard_map/all_gather | solution.py:13
  578.9 29.4 %all-gather.53.cloned.1.call-done = bf16[2048,256]{1,0:T(8,128)(2,1)} async-done(((bf16[512,256]{1,0:T(8,128)(2,1)}), bf16[2048,256]{1,0:T(8,128)(2,1)}) %all-gather.53.cloned.1.call-update) | async-done | bytes 1048592 | tf_op jit(solution)/shard_map/all_gather | solution.py:16
  611.7 25.5 %all-gather.59.cloned.1.call-done = bf16[2048,256]{1,0:T(8,128)(2,1)} async-done(((bf16[512,256]{1,0:T(8,128)(2,1)}), bf16[2048,256]{1,0:T(8,128)(2,1)}) %all-gather.59.cloned.1.call-update) | async-done | bytes 1048592 | tf_op jit(solution)/shard_map/all_gather | solution.py:16
  637.1 29.2 %all-gather.57.cloned.1.call-done = bf16[512,2048]{1,0:T(8,128)(2,1)} async-done(((bf16[512,256]{1,0:T(8,128)(2,1)}), bf16[512,2048]{1,0:T(8,128)(2,1)}) %all-gather.57.cloned.1.call-update) | async-done | bytes 2097168 | tf_op jit(solution)/shard_map/all_gather | solution.py:13
  670.5 26.1 %all-gather.63.cloned.1.call-done = bf16[2048,256]{1,0:T(8,128)(2,1)} async-done(((bf16[512,256]{1,0:T(8,128)(2,1)}), bf16[2048,256]{1,0:T(8,128)(2,1)}) %all-gather.63.cloned.1.call-update) | async-done | bytes 1048592 | tf_op jit(solution)/shard_map/all_gather | solution.py:16
  696.5 29.2 %all-gather.61.cloned.1.call-done = bf16[512,2048]{1,0:T(8,128)(2,1)} async-done(((bf16[512,256]{1,0:T(8,128)(2,1)}), bf16[512,2048]{1,0:T(8,128)(2,1)}) %all-gather.61.cloned.1.call-update) | async-done | bytes 2097168 | tf_op jit(solution)/shard_map/all_gather | solution.py:13
  730.4 25.9 %all-gather.55.cloned.1.call-done = bf16[512,2048]{1,0:T(8,128)(2,1)} async-done(((bf16[512,256]{1,0:T(8,128)(2,1)}), bf16[512,2048]{1,0:T(8,128)(2,1)}) %all-gather.55.cloned.1.call-update) | async-done | bytes 2097168 | tf_op jit(solution)/shard_map/all_gather | solution.py:13
  756.4 29.6 %all-gather.65.cloned.1.call-done = bf16[2048,256]{1,0:T(8,128)(2,1)} async-done(((bf16[512,256]{1,0:T(8,128)(2,1)}), bf16[2048,256]{1,0:T(8,128)(2,1)}) %all-gather.65.cloned.1.call-update) | async-done | bytes 1048592 | tf_op jit(solution)/shard_map/all_gather | solution.py:16
  789.3 25.6 %all-gather.71.cloned.1.call-done = bf16[2048,256]{1,0:T(8,128)(2,1)} async-done(((bf16[512,256]{1,0:T(8,128)(2,1)}), bf16[2048,256]{1,0:T(8,128)(2,1)}) %all-gather.71.cloned.1.call-update) | async-done | bytes 1048592 | tf_op jit(solution)/shard_map/all_gather | solution.py:16
  814.9 29.2 %all-gather.69.cloned.1.call-done = bf16[512,2048]{1,0:T(8,128)(2,1)} async-done(((bf16[512,256]{1,0:T(8,128)(2,1)}), bf16[512,2048]{1,0:T(8,128)(2,1)}) %all-gather.69.cloned.1.call-update) | async-done | bytes 2097168 | tf_op jit(solution)/shard_map/all_gather | solution.py:13
  848.1 26.2 %all-gather.75.cloned.1.call-done = bf16[2048,256]{1,0:T(8,128)(2,1)} async-done(((bf16[512,256]{1,0:T(8,128)(2,1)}), bf16[2048,256]{1,0:T(8,128)(2,1)}) %all-gather.75.cloned.1.call-update) | async-done | bytes 1048592 | tf_op jit(solution)/shard_map/all_gather | solution.py:16
  874.3 29.2 %all-gather.73.cloned.1.call-done = bf16[512,2048]{1,0:T(8,128)(2,1)} async-done(((bf16[512,256]{1,0:T(8,128)(2,1)}), bf16[512,2048]{1,0:T(8,128)(2,1)}) %all-gather.73.cloned.1.call-update) | async-done | bytes 2097168 | tf_op jit(solution)/shard_map/all_gather | solution.py:13
  906.9 27.1 %all-gather.67.cloned.1.call-done = bf16[512,2048]{1,0:T(8,128)(2,1)} async-done(((bf16[512,256]{1,0:T(8,128)(2,1)}), bf16[512,2048]{1,0:T(8,128)(2,1)}) %all-gather.67.cloned.1.call-update) | async-done | bytes 2097168 | tf_op jit(solution)/shard_map/all_gather | solution.py:13
  934.0 29.6 %all-gather.77.cloned.1.call-done = bf16[2048,256]{1,0:T(8,128)(2,1)} async-done(((bf16[512,256]{1,0:T(8,128)(2,1)}), bf16[2048,256]{1,0:T(8,128)(2,1)}) %all-gather.77.cloned.1.call-update) | async-done | bytes 1048592 | tf_op jit(solution)/shard_map/all_gather | solution.py:16
  967.6 40.3 %psum.71 = f32[]{:T(128)} all-reduce(f32[]{:T(128)} %get-tuple-element.3), channel_id=1, replica_groups=mesh['gx'=4,'gy'=8] {'gx','gy'}, use_global_device_ids=true, to_apply=%region_16.17 | all-reduce | flops 1 | bytes 8 | tf_op jit(solution)/shard_map/psum | solution.py:58
  1008.5 13.4 %all-reduce.1 = (f32[]{:T(128)}, f32[]{:T(128)}) all-reduce(f32[]{:T(128)} %get-tuple-element.4, f32[]{:T(128)} %get-tuple-element.13), channel_id=1, replica_groups=mesh['gx'=4,'gy'=8] {'gy'}, use_global_device_ids=true, to_apply=%region_10.11 | all-reduce | flops 2 | bytes 16 | tf_op jit(solution)/shard_map/psum | solution.py:7
  (91 shorter events, 72.6 us)
Async XLA Ops:
  7.2 137.7 %reduce-scatter.3.cloned.1.call-start = ((), (), s32[]{:S(2)}) async-start(), calls=%async_computation.2 | async-start | bytes 18874368 | tf_op jit(solution)/shard_map/reduce_scatter | solution.py:36
  26.0 118.9 %copy-start = (f32[512,256]{1,0:T(8,128)S(1)}, f32[512,256]{1,0:T(8,128)}, u32[]{:S(2)}) copy-start(f32[512,256]{1,0:T(8,128)} %param.7) | copy-start | bytes 1572868
  26.0 168.9 %reduce-scatter.5.cloned.1.call-start = ((), (), s32[]{:S(2)}) async-start(), calls=%async_computation.3 | async-start | bytes 2621440 | tf_op jit(solution)/shard_map/reduce_scatter | solution.py:37
  144.8 75.8 %all-gather.29.cloned.1.call-start = ((), (), s32[]{:S(2)}) async-start(), calls=%async_computation.5 | async-start | bytes 1310720 | tf_op jit(solution)/shard_map/all_gather | solution.py:16
  146.3 104.2 %all-gather.27.cloned.1.call-start = ((), (), s32[]{:S(2)}) async-start(), calls=%async_computation.4 | async-start | bytes 2359296 | tf_op jit(solution)/shard_map/all_gather | solution.py:13
  146.3 46.6 %copy-start.3 = (f32[2048]{0:T(1024)S(1)}, f32[2048]{0:T(1024)}, u32[]{:S(2)}) copy-start(f32[2048]{0:T(1024)} %param.6) | copy-start | bytes 24580
  194.1 59.6 %copy-start.2 = (f32[2048]{0:T(1024)}, f32[2048]{0:T(1024)S(1)}, u32[]{:S(2)}) copy-start(f32[2048]{0:T(1024)S(1)} %get-tuple-element.12) | copy-start | bytes 24580
  196.8 83.5 %all-gather.33.cloned.1.call-start = ((), (), s32[]{:S(2)}) async-start(), calls=%async_computation.7 | async-start | bytes 2359296 | tf_op jit(solution)/shard_map/all_gather | solution.py:13
  197.4 112.9 %all-gather.31.cloned.1.call-start = ((), (), s32[]{:S(2)}) async-start(), calls=%async_computation.6 | async-start | bytes 1310720 | tf_op jit(solution)/shard_map/all_gather | solution.py:16
  253.7 86.8 %all-gather.37.cloned.1.call-start = ((), (), s32[]{:S(2)}) async-start(), calls=%async_computation.9 | async-start | bytes 2359296 | tf_op jit(solution)/shard_map/all_gather | solution.py:13
  254.7 115.2 %all-gather.39.cloned.1.call-start = ((), (), s32[]{:S(2)}) async-start(), calls=%async_computation.10 | async-start | bytes 1310720 | tf_op jit(solution)/shard_map/all_gather | solution.py:16
  340.4 60.3 %all-gather.41.cloned.1.call-start = ((), (), s32[]{:S(2)}) async-start(), calls=%async_computation.11 | async-start | bytes 1310720 | tf_op jit(solution)/shard_map/all_gather | solution.py:16
  373.2 57.0 %all-gather.35.cloned.1.call-start = ((), (), s32[]{:S(2)}) async-start(), calls=%async_computation.8 | async-start | bytes 2359296 | tf_op jit(solution)/shard_map/all_gather | solution.py:13
  373.8 86.0 %all-gather.47.cloned.1.call-start = ((), (), s32[]{:S(2)}) async-start(), calls=%async_computation.14 | async-start | bytes 1310720 | tf_op jit(solution)/shard_map/all_gather | solution.py:16
  374.6 114.5 %all-gather.45.cloned.1.call-start = ((), (), s32[]{:S(2)}) async-start(), calls=%async_computation.13 | async-start | bytes 2359296 | tf_op jit(solution)/shard_map/all_gather | solution.py:13
  375.1 144.1 %all-gather.51.cloned.1.call-start = ((), (), s32[]{:S(2)}) async-start(), calls=%async_computation.16 | async-start | bytes 1310720 | tf_op jit(solution)/shard_map/all_gather | solution.py:16
  433.6 114.9 %all-gather.49.cloned.1.call-start = ((), (), s32[]{:S(2)}) async-start(), calls=%async_computation.15 | async-start | bytes 2359296 | tf_op jit(solution)/shard_map/all_gather | solution.py:13
  492.4 86.5 %all-gather.43.cloned.1.call-start = ((), (), s32[]{:S(2)}) async-start(), calls=%async_computation.12 | async-start | bytes 2359296 | tf_op jit(solution)/shard_map/all_gather | solution.py:13
  492.9 115.4 %all-gather.53.cloned.1.call-start = ((), (), s32[]{:S(2)}) async-start(), calls=%async_computation.17 | async-start | bytes 1310720 | tf_op jit(solution)/shard_map/all_gather | solution.py:16
  551.8 85.4 %all-gather.59.cloned.1.call-start = ((), (), s32[]{:S(2)}) async-start(), calls=%async_computation.20 | async-start | bytes 1310720 | tf_op jit(solution)/shard_map/all_gather | solution.py:16
  552.4 114.0 %all-gather.57.cloned.1.call-start = ((), (), s32[]{:S(2)}) async-start(), calls=%async_computation.19 | async-start | bytes 2359296 | tf_op jit(solution)/shard_map/all_gather | solution.py:13
  552.9 143.6 %all-gather.63.cloned.1.call-start = ((), (), s32[]{:S(2)}) async-start(), calls=%async_computation.22 | async-start | bytes 1310720 | tf_op jit(solution)/shard_map/all_gather | solution.py:16
  611.6 114.1 %all-gather.61.cloned.1.call-start = ((), (), s32[]{:S(2)}) async-start(), calls=%async_computation.21 | async-start | bytes 2359296 | tf_op jit(solution)/shard_map/all_gather | solution.py:13
  669.7 86.7 %all-gather.55.cloned.1.call-start = ((), (), s32[]{:S(2)}) async-start(), calls=%async_computation.18 | async-start | bytes 2359296 | tf_op jit(solution)/shard_map/all_gather | solution.py:13
  670.4 115.5 %all-gather.65.cloned.1.call-start = ((), (), s32[]{:S(2)}) async-start(), calls=%async_computation.23 | async-start | bytes 1310720 | tf_op jit(solution)/shard_map/all_gather | solution.py:16
  729.1 85.8 %all-gather.71.cloned.1.call-start = ((), (), s32[]{:S(2)}) async-start(), calls=%async_computation.26 | async-start | bytes 1310720 | tf_op jit(solution)/shard_map/all_gather | solution.py:16
  729.8 114.3 %all-gather.69.cloned.1.call-start = ((), (), s32[]{:S(2)}) async-start(), calls=%async_computation.25 | async-start | bytes 2359296 | tf_op jit(solution)/shard_map/all_gather | solution.py:13
  730.4 143.9 %all-gather.75.cloned.1.call-start = ((), (), s32[]{:S(2)}) async-start(), calls=%async_computation.28 | async-start | bytes 1310720 | tf_op jit(solution)/shard_map/all_gather | solution.py:16
  789.2 114.3 %all-gather.73.cloned.1.call-start = ((), (), s32[]{:S(2)}) async-start(), calls=%async_computation.27 | async-start | bytes 2359296 | tf_op jit(solution)/shard_map/all_gather | solution.py:13
  847.4 86.5 %all-gather.67.cloned.1.call-start = ((), (), s32[]{:S(2)}) async-start(), calls=%async_computation.24 | async-start | bytes 2359296 | tf_op jit(solution)/shard_map/all_gather | solution.py:13
  848.0 115.5 %copy-start.1 = (f32[512,256]{1,0:T(8,128)S(1)}, f32[512,256]{1,0:T(8,128)}, u32[]{:S(2)}) copy-start(f32[512,256]{1,0:T(8,128)} %reduce-scatter.5.cloned.1.call-done) | copy-start | bytes 1572868
  848.0 115.5 %all-gather.77.cloned.1.call-start = ((), (), s32[]{:S(2)}) async-start(), calls=%async_computation.29 | async-start | bytes 1310720 | tf_op jit(solution)/shard_map/all_gather | solution.py:16
Sparse Core Ops, SparseCore 0:
  26.1 118.6 reduce-scatter.2
  147.1 44.6 reduce-scatter.4
  193.4 27.1 all-gather.28
  222.9 27.4 all-gather.26
  252.2 28.0 all-gather.32
  282.3 27.9 all-gather.30
  312.2 27.5 all-gather.36
  341.9 27.9 all-gather.38
  373.4 27.3 all-gather.40
  403.1 27.1 all-gather.34
  431.8 27.9 all-gather.46
  461.6 27.4 all-gather.44
  491.2 27.9 all-gather.50
  521.0 27.4 all-gather.48
  550.8 28.0 all-gather.42
  580.3 27.9 all-gather.52
  609.8 27.3 all-gather.58
  638.9 27.4 all-gather.56
  668.5 27.9 all-gather.62
  698.3 27.4 all-gather.60
  728.2 28.0 all-gather.54
  757.9 27.9 all-gather.64
  787.5 27.3 all-gather.70
  816.6 27.4 all-gather.68
  846.3 27.9 all-gather.74
  876.0 27.4 all-gather.72
  905.9 28.0 all-gather.66
  935.6 27.9 all-gather.76
